TPU v7x, 32 devices: a whole 2x2x4 slice. The times are simulated.
32 devices in a mesh: dp: 2 (over x), tm: 4 (over z), mp: 4 (over y, core).
Axes of the slice: x: 2, y: 2, z: 4, core: 2. Of those that a mesh axis runs over, the one named last changes fastest.
Arguments:
- features: bfloat16 [32, 576, 1024], P(('dp', 'tm'), 'mp'), parts along dimension 0, may hold values from -6 to 6
- queries: bfloat16 [2048, 1024], P(('dp', 'tm')), parts along dimension 0, may hold values from -6 to 6
- anchor_frame: int32 [2048], P(('dp', 'tm')), parts along dimension 0, may hold values from 0 to 15, as said below
- anchor_patch: int32 [2048], P(('dp', 'tm')), parts along dimension 0, may hold values from 0 to 575
- time_offset: float32 [2048, 8, 4], P(('dp', 'tm')), parts along dimension 0, may hold values from -1.99 to 1.99
- space_offset: float32 [2, 2048, 8, 4], P(None, ('dp', 'tm')), parts along dimension 1, may hold values from -3 to 3
- value_weight: bfloat16 [1024, 1024], replicated, may hold values from -0.1875 to 0.1875
- point_weight: bfloat16 [1024, 32], replicated, may hold values from -0.1875 to 0.1875
- point_bias: float32 [32], replicated, may hold values from -6 to 260
- output_weight: bfloat16 [1024, 1024], P('mp'), may hold values from -0.1875 to 0.1875
- project_weight: bfloat16 [1024, 3584], P(None, 'mp'), may hold values from -2 to 2
- norm_gain: float32 [3584], P('mp'), may hold values from 0.1 to 1.9
- query_weight: bfloat16 [3584, 3072], P(None, 'mp'), may hold values from -0.09375 to 0.09375
- query_bias: float32 [3072], P('mp'), may hold values from -6 to 40
- cache_weight: bfloat16 [3584, 1024], P(None, 'mp'), may hold values from -0.09375 to 0.09375
- cache_bias: float32 [1024], P('mp'), may hold values from -6 to 40
Outputs:
- attention: bfloat16 [2048, 3072], P(('dp', 'tm'), 'mp'), parts along dimension 0
- key_value: bfloat16 [2048, 1024], P(('dp', 'tm'), 'mp'), parts along dimension 0
There are 2 independent parts, one for each index of `dp`. A program takes and returns all parts, laid end to end along the dimension named above; an argument that names none is the same for every part. Nothing has to cross between parts.
Inputs may be any that keep to these rules, and one draw needn't show every extreme that they name: `anchor_frame`: the anchor frame of query q lies among the 4 frames that begin at (q // 256) * 4.
All inputs are finite; a program needn't handle non-finite values.
Results may differ from a plain program's by a relative error of at most 0.04.
Values may be sent and summed in bfloat16 or wider, within the bound.
A program may use at most 64 MiB of HBM per device.

v0:
```python
import jax
import jax.numpy as jnp
from jax import lax
from jax.sharding import PartitionSpec as P

AH = 8
POINTS = 4
GRID = 24
KVH = 4
HD = 128
GROUP = 7


rope_base = 1000000.0
epsilon = 1e-06
masked = -1e30


def with_halo(block, sides, width):
    for axis, dim in sides:
        count = lax.axis_size(axis)
        forward = [(i, i + 1) for i in range(count - 1)]
        backward = [(target, source) for source, target in forward]
        low = lax.ppermute(
            lax.slice_in_dim(block, block.shape[dim] - width, None, axis=dim), axis, forward
        )
        high = lax.ppermute(lax.slice_in_dim(block, 0, width, axis=dim), axis, backward)
        block = jnp.concatenate([low, block, high], axis=dim)
    return block


def rotate(vectors, positions):
    half_width = vectors.shape[-1] // 2
    frequency = rope_base ** (-2.0 * jnp.arange(half_width, dtype=jnp.float32) / vectors.shape[-1])
    angles = positions.astype(jnp.float32)[:, None] * frequency[None, :]
    cosine = jnp.cos(angles)[:, None, :]
    sine_part = jnp.sin(angles)[:, None, :]
    first_half = vectors[..., :half_width]
    second_half = vectors[..., half_width:]
    return jnp.concatenate(
        [
            first_half * cosine - second_half * sine_part,
            second_half * cosine + first_half * sine_part,
        ],
        axis=-1,
    )


def trilinear_corners(frame_pos, row_pos, column_pos, weight, frame_total, side):
    floor_frame = jnp.floor(frame_pos)
    floor_row = jnp.floor(row_pos)
    floor_column = jnp.floor(column_pos)
    frame_part = frame_pos - floor_frame
    row_part = row_pos - floor_row
    column_part = column_pos - floor_column
    frame_start = floor_frame.astype(jnp.int32)
    row_start = floor_row.astype(jnp.int32)
    column_start = floor_column.astype(jnp.int32)
    listing = []
    for frame_step in (0, 1):
        for row_step in (0, 1):
            for column_step in (0, 1):
                frame_cell = frame_start + frame_step
                row_cell = row_start + row_step
                column_cell = column_start + column_step
                portion = weight * (frame_part if frame_step else 1.0 - frame_part)
                portion = portion * (row_part if row_step else 1.0 - row_part)
                portion = portion * (column_part if column_step else 1.0 - column_part)
                inside = (
                    (frame_cell >= 0)
                    & (frame_cell < frame_total)
                    & (row_cell >= 0)
                    & (row_cell < side)
                )
                inside = inside & (column_cell >= 0) & (column_cell < side)
                portion = jnp.where(inside, portion, 0.0)
                patch_id = jnp.clip(row_cell, 0, side - 1) * side + jnp.clip(
                    column_cell, 0, side - 1
                )
                listing.append((frame_cell, patch_id, portion))
    return listing


def make_attend(query_turned, positions, head_map, scaling):

    def attend(state_in, members, first_row):
        key_rows, value_rows = members
        length = key_rows.shape[0]
        block_len = 512
        block_count = length // block_len
        key_blocks = key_rows.reshape(block_count, block_len, -1, HD)[:, :, head_map, :]
        value_blocks = value_rows.reshape(block_count, block_len, -1, HD)[:, :, head_map, :]
        block_starts = jnp.arange(block_count, dtype=jnp.int32) * block_len

        def advance(running, inputs):
            peak_score, denominator, numerator = running
            key_block, value_block, block_start = inputs
            scores = (
                jnp.einsum(
                    "qhd,nhd->hqn", query_turned, key_block, preferred_element_type=jnp.float32
                )
                * scaling
            )
            key_pos = block_start + jnp.arange(block_len, dtype=jnp.int32)
            allowed = key_pos[None, None, :] <= positions[None, :, None]
            scores = jnp.where(allowed, scores, masked)
            new_peak = jnp.maximum(peak_score, jnp.max(scores, axis=-1))
            weights = jnp.where(allowed, jnp.exp(scores - new_peak[..., None]), 0.0)
            rescale = jnp.exp(peak_score - new_peak)
            denominator = denominator * rescale + jnp.sum(weights, axis=-1)
            numerator = numerator * rescale[..., None] + jnp.einsum(
                "hqn,nhd->hqd",
                weights.astype(jnp.bfloat16),
                value_block,
                preferred_element_type=jnp.float32,
            )
            return ((new_peak, denominator, numerator), None)

        result, unused = lax.scan(advance, state_in, (key_blocks, value_blocks, block_starts))
        return result

    return attend


def local(
    features,
    queries,
    anchor_frame,
    anchor_patch,
    time_offset,
    space_offset,
    value_weight,
    point_weight,
    point_bias,
    output_weight,
    project_weight,
    norm_gain,
    query_weight,
    query_bias,
    cache_weight,
    cache_bias,
):
    groups = lax.axis_size("mp")
    group_index = lax.axis_index("mp")
    frame_index = lax.axis_index("tm")
    frames_here, patches_here, feature_width = features.shape
    rows_here = queries.shape[0]
    frame_total = frames_here * lax.axis_size("tm")
    patch_total = GRID * GRID
    head_width = feature_width // AH
    heads_here = AH // groups
    first_frame = frame_index * frames_here - 2
    projected = jnp.dot(
        features.reshape(frames_here * patches_here, feature_width),
        value_weight,
        preferred_element_type=jnp.float32,
    )
    projected = projected.astype(jnp.bfloat16).reshape(frames_here, patches_here, feature_width)
    logits = jnp.dot(queries, point_weight, preferred_element_type=jnp.float32) + point_bias
    point_share = jax.nn.softmax(logits.reshape(rows_here, AH, POINTS), axis=-1)
    frame_pos = anchor_frame.astype(jnp.float32)[:, None, None] + time_offset
    row_pos = (anchor_patch // GRID).astype(jnp.float32)[:, None, None] + space_offset[0]
    column_pos = (anchor_patch % GRID).astype(jnp.float32)[:, None, None] + space_offset[1]

    def own_slice(array):
        return lax.dynamic_slice_in_dim(array, group_index * heads_here, heads_here, 1)

    by_head = lax.all_to_all(projected, "mp", split_axis=2, concat_axis=1, tiled=True)
    padded = with_halo(by_head, (("tm", 0),), 2)
    lookup = padded.reshape(-1, heads_here, head_width)
    head_lane = jnp.arange(heads_here, dtype=jnp.int32)[None, :, None]
    running = jnp.zeros((rows_here, heads_here, head_width), jnp.float32)
    for frame_cell, patch_id, portion in trilinear_corners(
        own_slice(frame_pos),
        own_slice(row_pos),
        own_slice(column_pos),
        own_slice(point_share),
        frame_total,
        GRID,
    ):
        local_frame = jnp.clip(frame_cell - first_frame, 0, frames_here + 3)
        picked = lookup[local_frame * patch_total + patch_id, head_lane]
        running = running + jnp.sum(portion[..., None] * picked.astype(jnp.float32), axis=2)
    sampled = running.reshape(rows_here, heads_here * head_width).astype(jnp.bfloat16)
    head_terms = jnp.dot(sampled, output_weight, preferred_element_type=jnp.float32)
    head_mix = lax.psum(head_terms, "mp")
    abstract = (queries.astype(jnp.float32) + head_mix).astype(jnp.bfloat16)
    visual = jnp.dot(abstract, project_weight, preferred_element_type=jnp.float32)
    squares = lax.psum(jnp.sum(visual * visual, axis=1), "mp")
    model_width = query_weight.shape[0]
    normed = (visual * lax.rsqrt(squares / model_width + epsilon)[:, None] * norm_gain).astype(
        jnp.bfloat16
    )
    shard_piece = lax.all_gather(normed, "mp", axis=1, tiled=True)
    query_sum = jnp.dot(shard_piece, query_weight, preferred_element_type=jnp.float32)
    cache_sum = jnp.dot(shard_piece, cache_weight, preferred_element_type=jnp.float32)
    positions = frame_index * rows_here + jnp.arange(rows_here, dtype=jnp.int32)
    query_heads = query_weight.shape[1] // HD
    query_turned = rotate(
        (query_sum + query_bias).reshape(rows_here, query_heads, HD), positions
    ).astype(jnp.bfloat16)
    cache_heads = cache_weight.shape[1] // HD
    cache_state = (cache_sum + cache_bias).reshape(rows_here, cache_heads, HD)
    is_key = group_index * cache_heads + jnp.arange(cache_heads, dtype=jnp.int32) < KVH
    cache_state = jnp.where(is_key[None, :, None], rotate(cache_state, positions), cache_state)
    key_value = cache_state.reshape(rows_here, cache_heads * HD).astype(jnp.bfloat16)
    cache_all = lax.all_gather(key_value, "mp", axis=1, tiled=True)
    key_rows = cache_all[:, : KVH * HD]
    value_rows = cache_all[:, KVH * HD :]
    own_heads = (group_index * query_heads + jnp.arange(query_heads, dtype=jnp.int32)) // GROUP
    scaling = HD ** (-0.5)
    initial = (
        jnp.full((query_heads, rows_here), masked, jnp.float32),
        jnp.zeros((query_heads, rows_here), jnp.float32),
        jnp.zeros((query_heads, rows_here, HD), jnp.float32),
    )
    span_heads = min(KVH, (query_heads - 1) // GROUP + 2)
    lowest = jnp.minimum(group_index * query_heads // GROUP, KVH - span_heads)
    key_rows = lax.dynamic_slice_in_dim(key_rows, lowest * HD, span_heads * HD, 1)
    value_rows = lax.dynamic_slice_in_dim(value_rows, lowest * HD, span_heads * HD, 1)
    attend = make_attend(query_turned, positions, own_heads - lowest, scaling)
    peak_score, denominator, numerator = attend(
        initial,
        (
            lax.all_gather(key_rows, "tm", axis=0, tiled=True),
            lax.all_gather(value_rows, "tm", axis=0, tiled=True),
        ),
        jnp.int32(0),
    )
    attention = (
        (numerator / denominator[..., None])
        .transpose(1, 0, 2)
        .reshape(rows_here, query_heads * HD)
        .astype(jnp.bfloat16)
    )
    return (attention, key_value)


def solution(mesh):
    return jax.shard_map(
        local,
        mesh=mesh,
        in_specs=(
            P(("dp", "tm"), "mp", None),
            P(("dp", "tm"), None),
            P(("dp", "tm")),
            P(("dp", "tm")),
            P(("dp", "tm"), None, None),
            P(None, ("dp", "tm"), None, None),
            P(),
            P(),
            P(),
            P("mp", None),
            P(None, "mp"),
            P("mp"),
            P(None, "mp"),
            P("mp"),
            P(None, "mp"),
            P("mp"),
        ),
        out_specs=(P(("dp", "tm"), "mp"), P(("dp", "tm"), "mp")),
        check_vma=False,
    )
```

profile of v0, /device:TPU:27, one launch (start us, length us, event | category | flops | bytes accessed | tf_op | source)
XLA Modules:
  0.0 493.7 jit_solution(2481878164457223012)
XLA Ops:
  8.8 2.7 convolution_convert_fusion
  14.0 5.2 %all-to-all-start = ((bf16[4,144,1024]{1,0,2:T(4,128)(2,1)}), bf16[4,144,1024]{1,0,2:T(4,128)(2,1)}, u32[]{:S(2)}, u32[]{:S(2)}) async-start(bf16[4,144,1024]{1,0,2:T(4,128)(2,1)} %copy.67), calls=%async_computation | async-start | bytes 4194304 | tf_op jit(solution)/shard_map/all_to_all | solution.py:168
  20.7 23.4 %all-to-all-done = bf16[4,144,1024]{1,0,2:T(4,128)(2,1)} async-done(((bf16[4,144,1024]{1,0,2:T(4,128)(2,1)}), bf16[4,144,1024]{1,0,2:T(4,128)(2,1)}, u32[]{:S(2)}, u32[]{:S(2)}) %all-to-all-start) | async-done | bytes 1179680 | tf_op jit(solution)/shard_map/all_to_all | solution.py:168
  44.0 4.7 fusion.73
  48.8 3.5 copy.68
  55.5 4.8 collective-permute-start.1
  70.7 3.1 copy.69
  73.9 2.9 pad_maximum_fusion
  76.8 5.7 %reshape.215 = bf16[4608,2,128]{2,1,0:T(2,128)(2,1)} reshape(bf16[8,576,256]{2,1,0:T(8,128)(2,1)} %pad_maximum_fusion) | data formatting | bytes 4718592 | tf_op jit(solution)/shard_map/reshape | solution.py:170
  82.5 32.6 %gather_fusion = bf16[2048,128]{1,0:T(8,128)(2,1)} fusion(bf16[4608,2,128]{2,1,0:T(2,128)(2,1)} %reshape.215, s32[2048]{0:T(1024)S(1)} %reshape.224), kind=kCustom, calls=%fused_computation | custom fusion | bytes 1064960 | tf_op jit(solution)/shard_map/gather | solution.py:182
  115.1 32.3 %gather_fusion.1 = bf16[2048,128]{1,0:T(8,128)(2,1)} fusion(bf16[4608,2,128]{2,1,0:T(2,128)(2,1)} %reshape.215, s32[2048]{0:T(1024)S(1)} %reshape.230), kind=kCustom, calls=%fused_computation.1 | custom fusion | bytes 1064960 | tf_op jit(solution)/shard_map/gather | solution.py:182
  147.5 32.4 %gather_fusion.2 = bf16[2048,128]{1,0:T(8,128)(2,1)} fusion(bf16[4608,2,128]{2,1,0:T(2,128)(2,1)} %reshape.215, s32[2048]{0:T(1024)S(1)} %reshape.236), kind=kCustom, calls=%fused_computation.2 | custom fusion | bytes 1064960 | tf_op jit(solution)/shard_map/gather | solution.py:182
  179.9 32.3 %gather_fusion.3 = bf16[2048,128]{1,0:T(8,128)(2,1)} fusion(bf16[4608,2,128]{2,1,0:T(2,128)(2,1)} %reshape.215, s32[2048]{0:T(1024)S(1)} %reshape.242), kind=kCustom, calls=%fused_computation.3 | custom fusion | bytes 1064960 | tf_op jit(solution)/shard_map/gather | solution.py:182
  212.2 32.6 %gather_fusion.4 = bf16[2048,128]{1,0:T(8,128)(2,1)} fusion(bf16[4608,2,128]{2,1,0:T(2,128)(2,1)} %reshape.215, s32[2048]{0:T(1024)S(1)} %reshape.248), kind=kCustom, calls=%fused_computation.4 | custom fusion | bytes 1064960 | tf_op jit(solution)/shard_map/gather | solution.py:182
  244.8 32.4 %gather_fusion.5 = bf16[2048,128]{1,0:T(8,128)(2,1)} fusion(bf16[4608,2,128]{2,1,0:T(2,128)(2,1)} %reshape.215, s32[2048]{0:T(1024)S(1)} %reshape.254), kind=kCustom, calls=%fused_computation.5 | custom fusion | bytes 1064960 | tf_op jit(solution)/shard_map/gather | solution.py:182
  277.2 23.0 %gather_fusion.6 = bf16[2048,128]{1,0:T(8,128)(2,1)S(1)} fusion(bf16[4608,2,128]{2,1,0:T(2,128)(2,1)} %reshape.215, s32[2048]{0:T(1024)S(1)} %reshape.260), kind=kCustom, calls=%fused_computation.6 | custom fusion | bytes 1064960 | tf_op jit(solution)/shard_map/gather | solution.py:182
  300.2 23.1 %gather_fusion.7 = bf16[2048,128]{1,0:T(8,128)(2,1)S(1)} fusion(bf16[4608,2,128]{2,1,0:T(2,128)(2,1)} %reshape.215, s32[2048]{0:T(1024)S(1)} %reshape.266), kind=kCustom, calls=%fused_computation.7 | custom fusion | bytes 1064960 | tf_op jit(solution)/shard_map/gather | solution.py:182
  323.3 3.7 fusion.28
  327.0 3.3 fusion.26
  336.4 37.8 %all-reduce.2.cloned.1.call-done = f32[256,1024]{1,0:T(8,128)} async-done(((f32[256,1024]{1,0:T(8,128)}), f32[256,1024]{1,0:T(8,128)}) %all-reduce.2.cloned.1.call-update) | async-done | bytes 1048592 | tf_op jit(solution)/shard_map/psum | solution.py:186
  376.9 6.3 %psum.15 = f32[256]{0:T(256)S(1)} all-reduce(f32[256]{0:T(256)S(1)} %get-tuple-element.180), channel_id=1, replica_groups=mesh['dp'=2,'tm'=4,'mp'=4] {'mp'}, use_global_device_ids=true, to_apply=%region_12.13 | all-reduce | flops 256 | bytes 2048 | tf_op jit(solution)/shard_map/psum | solution.py:189
  385.8 20.4 %all-gather.2.cloned.1.call-done = bf16[256,3584]{1,0:T(8,128)(2,1)} async-done(((bf16[256,896]{1,0:T(8,128)(2,1)}), bf16[256,3584]{1,0:T(8,128)(2,1)}) %all-gather.2.cloned.1.call-update) | async-done | bytes 1835024 | tf_op jit(solution)/shard_map/all_gather | solution.py:194
  406.3 2.9 convolution_add_fusion.1
  409.3 7.3 %all_gather.13 = bf16[256,1024]{0,1:T(8,128)(2,1)S(1)} all-gather(bf16[256,256]{0,1:T(8,128)(2,1)S(1)} %fusion.31), channel_id=1, replica_groups=mesh['dp'=2,'tm'=4,'mp'=4] {'mp'}, dimensions={1}, use_global_device_ids=true | all-gather | bytes 655360 | tf_op jit(solution)/shard_map/all_gather | solution.py:207
  417.4 5.6 %convolution_add_fusion = f32[256,768]{1,0:T(8,128)} fusion(bf16[256,3584]{1,0:T(8,128)(2,1)} %all-gather.2.cloned.1.call-done, bf16[3584,768]{1,0:T(8,128)(2,1)} %param.30, f32[768]{0:T(1024)S(1)} %copy-done.23), kind=kOutput, calls=%fused_computation.39 | convolution fusion | flops 1409482752 | bytes 8129536 | tf_op jit(solution)/shard_map/dot_general | solution.py:195
  425.5 13.1 %all_gather.15 = bf16[1024,256]{0,1:T(8,128)(2,1)S(1)} all-gather(bf16[256,256]{0,1:T(8,128)(2,1)S(1)} %constant_dynamic-slice_fusion), channel_id=1, replica_groups=mesh['dp'=2,'tm'=4,'mp'=4] {'tm'}, dimensions={0}, use_global_device_ids=true | all-gather | bytes 655360 | tf_op jit(solution)/shard_map/all_gather | solution.py:226
  440.4 13.7 %all_gather.14 = bf16[1024,256]{0,1:T(8,128)(2,1)S(1)} all-gather(bf16[256,256]{0,1:T(8,128)(2,1)S(1)} %constant_dynamic-slice_fusion.1), channel_id=1, replica_groups=mesh['dp'=2,'tm'=4,'mp'=4] {'tm'}, dimensions={0}, use_global_device_ids=true | all-gather | bytes 655360 | tf_op jit(solution)/shard_map/all_gather | solution.py:225
  460.8 23.6 %while.15 = (s32[]{:T(128)}, f32[6,256]{1,0:T(8,128)S(1)}, f32[6,256]{1,0:T(8,128)S(1)}, f32[6,256,128]{2,1,0:T(8,128)}, s32[2]{0:T(128)}, /*index=5*/bf16[2,512...) while((s32[]{:T(128)}, f32[6,256]{1,0:T(8,128)S(1)}, ...), condition=%wide.region_16.17_spmd.clone, body=%wide.region_13.16_spmd.clone.sunk | while | flops 413606144 | bytes 32480480 | solution.py:119
  462.8 3.5 fusion.96
  466.3 2.8 fusion.97
  474.6 3.5 fusion.96
  478.1 2.8 fusion.97
  (154 shorter events, 55.3 us)
Async XLA Ops:
  7.2 1.6 copy-start
  13.9 5.3 %copy-start.2 = (bf16[256,1024]{1,0:T(8,128)(2,1)S(1)}, bf16[256,1024]{1,0:T(8,128)(2,1)}, u32[]{:S(2)}) copy-start(bf16[256,1024]{1,0:T(8,128)(2,1)} %param.19) | copy-start | bytes 1572868
  14.0 5.3 %copy-start.17 = (bf16[1024,32]{0,1:T(8,128)(2,1)S(1)}, bf16[1024,32]{0,1:T(8,128)(2,1)}, u32[]{:S(2)}) copy-start(bf16[1024,32]{0,1:T(8,128)(2,1)} %param.25) | copy-start | bytes 196612
  14.0 5.3 %copy-start.22 = (f32[32]{0:T(128)S(1)}, f32[32]{0:T(128)}, u32[]{:S(2)}) copy-start(f32[32]{0:T(128)} %param.26) | copy-start | bytes 388
  14.0 5.6 %copy-start.21 = (s32[256]{0:T(256)S(1)}, s32[256]{0:T(256)}, u32[]{:S(2)}) copy-start(s32[256]{0:T(256)} %param.20) | copy-start | bytes 3076
  14.0 5.7 %copy-start.20 = (s32[256]{0:T(256)S(1)}, s32[256]{0:T(256)}, u32[]{:S(2)}) copy-start(s32[256]{0:T(256)} %param.21) | copy-start | bytes 3076
  14.0 5.7 %copy-start.16 = (f32[2,256,8,4]{1,3,2,0:T(4,128)S(1)}, f32[2,256,8,4]{1,3,2,0:T(4,128)}, u32[]{:S(2)}) copy-start(f32[2,256,8,4]{1,3,2,0:T(4,128)} %param.23) | copy-start | bytes 196612
  14.0 5.7 %copy-start.18 = (f32[256,8,4]{0,2,1:T(4,128)S(1)}, f32[256,8,4]{0,2,1:T(4,128)}, u32[]{:S(2)}) copy-start(f32[256,8,4]{0,2,1:T(4,128)} %param.22) | copy-start | bytes 98308
  14.0 30.0 %all-to-all-start = ((bf16[4,144,1024]{1,0,2:T(4,128)(2,1)}), bf16[4,144,1024]{1,0,2:T(4,128)(2,1)}, u32[]{:S(2)}, u32[]{:S(2)}) async-start(bf16[4,144,1024]{1,0,2:T(4,128)(2,1)} %copy.67), calls=%async_computation | async-start | bytes 4194304 | tf_op jit(solution)/shard_map/all_to_all | solution.py:168
  19.2 355.1 %all-reduce.2.cloned.1.call-start = ((), (), s32[]{:S(2)}) async-start(), calls=%async_computation.1 | async-start | bytes 2097152 | tf_op jit(solution)/shard_map/psum | solution.py:186
  52.3 21.6 %collective-permute-start = (bf16[2,576,256]{2,1,0:T(8,128)(2,1)}, bf16[2,576,256]{2,1,0:T(8,128)(2,1)}, u32[]{:S(2)}, u32[]{:S(2)}) collective-permute-start(bf16[2,576,256]{2,1,0:T(8,128)(2,1)} %bitcast.167), channel_id=1, source_target_pairs={{0,4},{4,8},{8,12},{1,5},{5,9},{9,13},{2,6},{6,10},{10,14},{3,7},{... | collective-permute-start | bytes 1769480 | tf_op jit(solution)/shard_map/ppermute | solution.py:24
  55.5 18.4 %collective-permute-start.1 = (bf16[2,576,256]{2,1,0:T(8,128)(2,1)}, bf16[2,576,256]{2,1,0:T(8,128)(2,1)}, u32[]{:S(2)}, u32[]{:S(2)}) collective-permute-start(bf16[2,576,256]{2,1,0:T(8,128)(2,1)} %bitcast.168), channel_id=1, source_target_pairs={{4,0},{8,4},{12,8},{5,1},{9,5},{13,9},{6,2},{10,6},{14,10},{7,3},{... | collective-permute-start | bytes 1769480 | tf_op jit(solution)/shard_map/ppermute | solution.py:27
  300.2 23.2 %copy-start.8 = (f32[256,2,4]{2,1,0:T(2,128)S(1)}, f32[256,2,4]{2,1,0:T(2,128)}, u32[]{:S(2)}) copy-start(f32[256,2,4]{2,1,0:T(2,128)} %copy.66) | copy-start | bytes 24580
  323.2 3.8 copy-start.6
  323.3 3.8 copy-start.7
  323.3 7.0 %copy-start.4 = (bf16[2048,128]{1,0:T(8,128)(2,1)S(1)}, bf16[2048,128]{1,0:T(8,128)(2,1)}, u32[]{:S(2)}) copy-start(bf16[2048,128]{1,0:T(8,128)(2,1)} %gather_fusion.4) | copy-start | bytes 1572868
  323.3 7.0 %copy-start.5 = (bf16[2048,128]{1,0:T(8,128)(2,1)S(1)}, bf16[2048,128]{1,0:T(8,128)(2,1)}, u32[]{:S(2)}) copy-start(bf16[2048,128]{1,0:T(8,128)(2,1)} %gather_fusion.5) | copy-start | bytes 1572868
  323.3 7.0 %copy-start.9 = (f32[256,2,4]{2,1,0:T(2,128)S(1)}, f32[256,2,4]{2,1,0:T(2,128)}, u32[]{:S(2)}) copy-start(f32[256,2,4]{2,1,0:T(2,128)} %copy.80) | copy-start | bytes 24580
  323.3 7.0 %copy-start.10 = (f32[256,2,4]{2,1,0:T(2,128)S(1)}, f32[256,2,4]{2,1,0:T(2,128)}, u32[]{:S(2)}) copy-start(f32[256,2,4]{2,1,0:T(2,128)} %copy.78) | copy-start | bytes 24580
  327.0 5.4 %copy-start.11 = (f32[256,2,4]{2,1,0:T(2,128)S(1)}, f32[256,2,4]{2,1,0:T(2,128)}, u32[]{:S(2)}) copy-start(f32[256,2,4]{2,1,0:T(2,128)} %copy.82) | copy-start | bytes 24580
  327.0 5.4 %copy-start.12 = (f32[256,2,4]{2,1,0:T(2,128)S(1)}, f32[256,2,4]{2,1,0:T(2,128)}, u32[]{:S(2)}) copy-start(f32[256,2,4]{2,1,0:T(2,128)} %copy.84) | copy-start | bytes 24580
  332.3 2.5 copy-start.15
  334.4 39.9 %copy-start.3 = (bf16[256,1024]{1,0:T(8,128)(2,1)S(1)}, bf16[256,1024]{1,0:T(8,128)(2,1)}, u32[]{:S(2)}) copy-start(bf16[256,1024]{1,0:T(8,128)(2,1)} %param.19) | copy-start | bytes 1572868
  336.2 47.0 %copy-start.19 = (f32[896]{0:T(1024)S(1)}, f32[896]{0:T(1024)}, u32[]{:S(2)}) copy-start(f32[896]{0:T(1024)} %param.29) | copy-start | bytes 10756
  336.2 70.1 %all-gather.2.cloned.1.call-start = ((), (), s32[]{:S(2)}) async-start(), calls=%async_computation.2 | async-start | bytes 2293760 | tf_op jit(solution)/shard_map/all_gather | solution.py:194
  385.8 31.6 %copy-start.23 = (f32[768]{0:T(1024)S(1)}, f32[768]{0:T(1024)}, u32[]{:S(2)}) copy-start(f32[768]{0:T(1024)} %param.31) | copy-start | bytes 9220
  462.8 6.3 %copy-start.13 = (f32[6,256,128]{2,1,0:T(8,128)S(1)}, f32[6,256,128]{2,1,0:T(8,128)}, u32[]{:S(2)}) copy-start(f32[6,256,128]{2,1,0:T(8,128)} %get-tuple-element.267) | copy-start | bytes 2359300 | tf_op jit(solution)/shard_map/while
  466.3 2.8 copy-start.1
  471.7 0.9 copy-start.14
  474.6 6.3 %copy-start.13 = (f32[6,256,128]{2,1,0:T(8,128)S(1)}, f32[6,256,128]{2,1,0:T(8,128)}, u32[]{:S(2)}) copy-start(f32[6,256,128]{2,1,0:T(8,128)} %get-tuple-element.267) | copy-start | bytes 2359300 | tf_op jit(solution)/shard_map/while
  478.1 2.8 copy-start.1
  483.5 0.9 copy-start.14
Sparse Core Ops, SparseCore 0:
  336.3 37.9 all-reduce.1
  384.3 21.9 all-gather.1
where the time goes:
time: 502 us; the launch traced here: 494 us
  local copies, waits for them, and re-layouts  293 us (58%)
  waiting for transfers between devices  81.7 us (16%)
  blocking collectives  40.3 us (8%)
  matrix products  27.4 us (5%)
  other arithmetic  24.5 us (5%)
  between operations  14.7 us (3%)
  starting transfers between devices  11.6 us (2%)
    gather x8, local copies, waits for them, and re-layouts, local(): picked = lookup[local_frame * patch_total + patch_id, head_lane]  241 us
    psum x1, waiting for transfers between devices, local(): head_mix = lax.psum(head_terms, 'mp')  37.8 us
    all_to_all x1, waiting for transfers between devices, local(): lax.all_to_all(projected, 'mp', split_axis=2, concat_axis=1, tiled=True)  23.4 us
    all_gather x1, waiting for transfers between devices, local(): shard_piece = lax.all_gather(normed, 'mp', axis=1, tiled=True)  20.4 us
    all_gather x1, blocking collectives, local(): lax.all_gather(key_rows, 'tm', axis=0, tiled=True)  13.7 us
    all_gather x1, blocking collectives, local(): lax.all_gather(value_rows, 'tm', axis=0, tiled=True)  13.1 us
    reduce_sum x4, other arithmetic, local(): jnp.sum(portion[..., None] * picked.astype(jnp.float32), axis=2)  10.9 us
  transfers between devices with their start and end apart: 5, of which 3 were waited for; matrix products, arithmetic and copies ran while one was open for 4% of the time, Pallas kernels for 0%

commit v1 on v0

v1 whole, which is shorter than its diff:
```python
import functools

import jax
import jax.numpy as jnp
from jax import lax
from jax.experimental import pallas as pl
from jax.experimental.pallas import tpu as pltpu
from jax.sharding import PartitionSpec as P

AH = 8
POINTS = 4
GRID = 24
KVH = 4
HD = 128
GROUP = 7

rope_base = 1000000.0
epsilon = 1e-06
masked = -1e30
MESH = pl.DeviceIdType.MESH
BF = jnp.bfloat16
F32 = jnp.float32


def remote(src, dst, send, recv, device):
    return pltpu.make_async_remote_copy(
        src_ref=src, dst_ref=dst, send_sem=send, recv_sem=recv, device_id=device, device_id_type=MESH
    )


class Gather:
    def __init__(self, slot_ref, own, sems, groups, me):
        self.chips = groups // 2
        self.chip, self.core = me // 2, me % 2
        self.me, self.partner = me, me + 1 - 2 * (me % 2)
        cs, cr, ps, pr = sems
        self.cross = [None] + [
            remote(
                own,
                slot_ref(me),
                cs(d),
                cr(d),
                {"mp": (self.chip + d) % self.chips * 2 + self.core},
            )
            for d in range(1, self.chips)
        ]
        self.near = [remote(own, slot_ref(me), ps(0), pr(0), {"mp": self.partner})]
        for d in range(1, self.chips):
            slot = slot_ref(self.slot(d, self.core))
            self.near.append(remote(slot, slot, ps(d), pr(d), {"mp": self.partner}))

    def slot(self, d, core):
        return (self.chip + self.chips - d) % self.chips * 2 + core

    def start(self):
        for copy in self.cross[1:]:
            copy.start()
        self.near[0].start()

    def arrivals(self):
        self.near[0].wait_recv()
        yield self.partner
        for d in range(1, self.chips):
            self.cross[d].wait_recv()
            self.near[d].start()
            yield self.slot(d, self.core)
            self.near[d].wait_recv()
            yield self.slot(d, 1 - self.core)

    def drain(self):
        for copy in self.cross[1:] + self.near:
            copy.wait_send()


def kernel(
    groups,
    spans,
    frames,
    features,
    queries,
    coords,
    cosine,
    sine,
    gain,
    query_bias,
    cache_bias,
    value_hbm,
    output_hbm,
    project_hbm,
    query_hbm,
    cache_hbm,
    attention,
    key_value,
    vw,
    wo,
    wp,
    wq,
    wc,
    halo,
    own_values,
    halo_values,
    corner,
    partial,
    rs_send,
    rs_recv,
    ab,
    vx,
    ssq,
    q_acc,
    kv_acc,
    qs,
    kv,
    peak,
    denom,
    numer,
    load_sem,
    halo_send,
    halo_recv,
    rs_ss,
    rs_rs,
    sq_ss,
    sq_rs,
    z_ss,
    z_rs,
    ag_sem,
):
    me = lax.axis_index("mp")
    t = lax.axis_index("tm")
    cells, width = features.shape
    rows = queries.shape[0]
    half = 2 * (cells // frames)
    lines = cells // frames // GRID
    piece = rows // groups
    model = wp.shape[1]
    q_heads = qs.shape[0]
    ch = kv.shape[3] // HD

    loads = [
        pltpu.make_async_copy(src, dst, load_sem.at[i])
        for i, (src, dst) in enumerate(
            [
                (value_hbm, vw),
                (output_hbm, wo.at[me]),
                (project_hbm, wp),
                (cache_hbm, wc),
                (query_hbm, wq),
            ]
        )
    ]
    for load in loads:
        load.start()

    barrier = pltpu.get_barrier_semaphore()
    for d in range(1, groups):
        pl.semaphore_signal(barrier, inc=1, device_id={"mp": (me + d) % groups}, device_id_type=MESH)
    for d in range(1, spans):
        pl.semaphore_signal(barrier, inc=1, device_id={"tm": (t + d) % spans}, device_id_type=MESH)
    pl.semaphore_wait(barrier, groups + spans - 2)

    low, high = halo.at[pl.ds(0, half)], halo.at[pl.ds(half, half)]
    up = remote(
        features.at[pl.ds(cells - half, half)], low, halo_send.at[0], halo_recv.at[0], {"tm": (t + 1) % spans}
    )
    down = remote(
        features.at[pl.ds(0, half)],
        high,
        halo_send.at[1],
        halo_recv.at[1],
        {"tm": (t + spans - 1) % spans},
    )

    @pl.when(t < spans - 1)
    def _():
        up.start()

    @pl.when(t > 0)
    def _():
        down.start()

    @pl.when(t == 0)
    def _():
        halo[pl.ds(0, half), :] = jnp.zeros((half, width), BF)

    @pl.when(t == spans - 1)
    def _():
        halo[pl.ds(half, half), :] = jnp.zeros((half, width), BF)

    def gather_sems(index):
        return [functools.partial(lambda k, d: ag_sem.at[index, k, d], k) for k in range(4)]

    wo_gather = Gather(lambda s: wo.at[s], output_hbm, gather_sems(0), groups, me)
    wo_gather.start()

    loads[0].wait()

    def project_values(source, target):
        @pl.loop(0, width // 256)
        def _(c):
            cols = pl.ds(pl.multiple_of(c * 256, 256), 256)
            target[:, cols] = jnp.dot(
                source[...], vw[:, cols], preferred_element_type=F32
            ).astype(BF)

    line_index = lax.broadcasted_iota(jnp.int32, (GRID, rows), 0).astype(F32)
    first_line = (me * lines).astype(F32)
    first_frame = (t * frames).astype(F32)

    def hat(position, cell):
        return jnp.maximum(1.0 - jnp.abs(position - cell), 0.0)

    def sample(values, offsets, head):
        info = coords[head]
        columns = [hat(info[8 + k : 9 + k], line_index) for k in range(POINTS)]
        for f, offset in enumerate(offsets):
            timed = info[12:16] * hat(info[0:4], first_frame + offset)
            for line in range(lines):
                share = timed * hat(info[4:8], first_line + line)
                total = share[0:1] * columns[0]
                for k in range(1, POINTS):
                    total = total + share[k : k + 1] * columns[k]
                corner[pl.ds((f * lines + line) * GRID, GRID), :] = total
        cols = pl.ds(pl.multiple_of(head * HD, HD), HD)
        return lax.dot_general(
            corner[pl.ds(0, values.shape[0]), :].astype(BF),
            values[:, cols],
            (((0,), (0,)), ((), ())),
            preferred_element_type=F32,
        )

    project_values(features, own_values)

    @pl.loop(0, AH)
    def _(head):
        cols = pl.ds(pl.multiple_of(head * HD, HD), HD)
        partial[:, cols] = sample(own_values, range(frames), head)

    @pl.when(t > 0)
    def _():
        up.wait_recv()

    @pl.when(t < spans - 1)
    def _():
        down.wait_recv()

    project_values(halo, halo_values)

    @pl.loop(0, AH)
    def _(head):
        cols = pl.ds(pl.multiple_of(head * HD, HD), HD)
        total = partial[:, cols] + sample(halo_values, (-2, -1, frames, frames + 1), head)
        rs_send[:, :, cols] = total.reshape(groups, piece, HD).astype(BF)

    rs = []
    for d in range(1, groups):
        peer = (me + d) % groups
        copy = remote(rs_send.at[peer], rs_recv.at[d], rs_ss.at[d], rs_rs.at[d], {"mp": peer})
        copy.start()
        rs.append(copy)

    loads[1].wait()
    for _ in wo_gather.arrivals():
        pass

    total = rs_send[me].astype(F32)
    for d in range(1, groups):
        rs[d - 1].wait_recv()
        total = total + rs_recv[d].astype(F32)
    mixed = jnp.dot(total.astype(BF), wo[...].reshape(width, width), preferred_element_type=F32)
    own_rows = pl.ds(pl.multiple_of(me * piece, piece), piece)
    ab[me] = (queries[own_rows, :].astype(F32) + mixed).astype(BF)
    ab_gather = Gather(lambda s: ab.at[s], ab.at[me], gather_sems(1), groups, me)
    ab_gather.start()
    loads[2].wait()
    for _ in ab_gather.arrivals():
        pass

    visual = jnp.dot(ab[...].reshape(rows, width), wp[...], preferred_element_type=F32)
    vx[me] = (visual * gain[...]).astype(BF)
    vx_gather = Gather(lambda s: vx.at[s], vx.at[me], gather_sems(2), groups, me)
    vx_gather.start()
    squares = jnp.broadcast_to(jnp.sum(visual * visual, axis=1, keepdims=True), (rows, HD)).T
    ssq[0] = squares[0:8]
    sq = []
    for d in range(1, groups):
        copy = remote(
            ssq.at[0], ssq.at[d], sq_ss.at[d], sq_rs.at[d], {"mp": (me + d) % groups}
        )
        copy.start()
        sq.append(copy)

    q_width = wq.shape[1]
    tile = 256 if q_width % 256 == 0 else 128

    def slot_rows(slot):
        return pl.ds(pl.multiple_of(slot * model, 64), model)

    def add_cache(slot, first):
        term = jnp.dot(vx[slot], wc[slot_rows(slot), :], preferred_element_type=F32)
        kv_acc[...] = term if first else kv_acc[...] + term

    def add_query(slot, first):
        @pl.loop(0, q_width // tile)
        def _(c):
            cols = pl.ds(pl.multiple_of(c * tile, tile), tile)
            term = jnp.dot(vx[slot], wq[slot_rows(slot), cols], preferred_element_type=F32)
            q_acc[:, cols] = term if first else q_acc[:, cols] + term

    loads[3].wait()
    loads[4].wait()
    add_cache(me, True)
    add_query(me, True)
    for order, slot in enumerate(vx_gather.arrivals()):
        add_cache(slot, False)
        if order < groups - 2:
            add_query(slot, False)
        last = slot

    square_sum = ssq[0]
    for d in range(1, groups):
        sq[d - 1].wait_recv()
        square_sum = square_sum + ssq[d]
    scale_row = lax.rsqrt(square_sum * (1.0 / (model * groups)) + epsilon)
    scale = jnp.broadcast_to(scale_row[0:1], (HD, rows)).T

    def turn(x, cos, sin):
        return x * cos + pltpu.roll(x, HD // 2, 1) * sin

    for i in range(ch):
        is_key = me * ch + i < KVH
        cols = slice(i * HD, (i + 1) * HD)
        state = kv_acc[:, cols] * scale + cache_bias[:, cols]
        cos = jnp.where(is_key, cosine[...], 1.0)
        sin = jnp.where(is_key, sine[...], 0.0)
        state = turn(state, cos, sin).astype(BF)
        kv[t, me, :, cols] = state
        key_value[:, cols] = state

    mine = kv.at[t, me]
    z_copies = []
    for d in range(1, spans):
        z_copies.append(remote(mine, mine, z_ss.at[d], z_rs.at[d], {"tm": (t + d) % spans}))

        @pl.when(t + d < spans)
        def _(d=d):
            z_copies[d - 1].start()

    def block_gather(d):
        j = lax.rem(t + spans - d, spans)
        return j, Gather(lambda s: kv.at[j, s], kv.at[j, me], gather_sems(3 + d), groups, me)

    own_gather = block_gather(0)
    own_gather[1].start()
    add_query(last, False)
    for i in range(q_heads):
        cols = slice(i * HD, (i + 1) * HD)
        state = q_acc[:, cols] * scale + query_bias[:, cols]
        qs[i] = turn(state, cosine[...], sine[...]).astype(BF)

    def attend(j, diagonal):
        @pl.loop(0, q_heads)
        def _(i):
            g = (me * q_heads + i) // GROUP
            k_cols = pl.ds(pl.multiple_of(lax.rem(g, ch) * HD, HD), HD)
            keys = kv[j, g // ch, :, k_cols]
            values = kv[j, (KVH + g) // ch, :, pl.ds(pl.multiple_of(lax.rem(KVH + g, ch) * HD, HD), HD)]
            scores = lax.dot_general(
                qs[i], keys, (((1,), (1,)), ((), ())), preferred_element_type=F32
            ) * (HD ** -0.5)
            if diagonal:
                q_pos = lax.broadcasted_iota(jnp.int32, (rows, rows), 0)
                k_pos = lax.broadcasted_iota(jnp.int32, (rows, rows), 1)
                scores = jnp.where(k_pos <= q_pos, scores, masked)
            top = jnp.max(scores, axis=1, keepdims=True)
            if diagonal:
                new_peak = jnp.broadcast_to(top, (rows, HD))
            else:
                new_peak = jnp.maximum(peak[i], top)
            weights = jnp.exp(scores - new_peak[:, 0:1])
            added = jnp.sum(weights, axis=1, keepdims=True)
            product = jnp.dot(weights.astype(BF), values, preferred_element_type=F32)
            if diagonal:
                denom[i] = jnp.broadcast_to(added, (rows, HD))
                numer[i] = product
            else:
                rescale = jnp.exp(peak[i] - new_peak)
                denom[i] = denom[i] * rescale + added
                numer[i] = numer[i] * rescale + product
            peak[i] = new_peak

    for _ in own_gather[1].arrivals():
        pass
    attend(t, True)
    for d in range(1, spans):

        @pl.when(t >= d)
        def _(d=d):
            j, gather = block_gather(d)
            arrived = kv.at[j, me]
            remote(arrived, arrived, z_ss.at[d], z_rs.at[d], {"tm": t}).wait_recv()
            gather.start()
            for _ in gather.arrivals():
                pass
            attend(j, False)
            gather.drain()

    for i in range(q_heads):
        attention[:, i * HD : (i + 1) * HD] = (numer[i] / denom[i]).astype(BF)

    @pl.when(t < spans - 1)
    def _():
        up.wait_send()

    @pl.when(t > 0)
    def _():
        down.wait_send()

    for gather in (wo_gather, ab_gather, vx_gather, own_gather[1]):
        gather.drain()
    for copy in rs + sq:
        copy.wait_send()
    for d in range(1, spans):

        @pl.when(t + d < spans)
        def _(d=d):
            z_copies[d - 1].wait_send()


def local(
    features,
    queries,
    anchor_frame,
    anchor_patch,
    time_offset,
    space_offset,
    value_weight,
    point_weight,
    point_bias,
    output_weight,
    project_weight,
    norm_gain,
    query_weight,
    query_bias,
    cache_weight,
    cache_bias,
):
    groups = lax.axis_size("mp")
    spans = lax.axis_size("tm")
    frames_here, patches_here, width = features.shape
    cells = frames_here * patches_here
    rows = queries.shape[0]
    logits = jnp.dot(queries, point_weight, preferred_element_type=F32) + point_bias
    share = jax.nn.softmax(logits.reshape(rows, AH, POINTS), axis=-1)
    frame_pos = anchor_frame.astype(F32)[:, None, None] + time_offset
    row_pos = (anchor_patch // GRID).astype(F32)[:, None, None] + space_offset[0]
    column_pos = (anchor_patch % GRID).astype(F32)[:, None, None] + space_offset[1]
    coords = jnp.stack([frame_pos, row_pos, column_pos, share], axis=0)
    coords = coords.transpose(2, 0, 3, 1).reshape(AH, 4 * POINTS, rows)
    positions = lax.axis_index("tm") * rows + jnp.arange(rows, dtype=jnp.int32)
    frequency = rope_base ** (-2.0 * jnp.arange(HD // 2, dtype=F32) / HD)
    angles = positions.astype(F32)[:, None] * frequency[None, :]
    cosine = jnp.cos(angles)
    sine = jnp.sin(angles)
    cosine = jnp.concatenate([cosine, cosine], axis=1)
    sine = jnp.concatenate([-sine, sine], axis=1)
    model = project_weight.shape[1]
    q_width = query_weight.shape[1]
    c_width = cache_weight.shape[1]
    q_heads = q_width // HD
    piece = rows // groups
    chips = groups // 2
    vmem = pl.BlockSpec(memory_space=pltpu.VMEM)
    hbm = pl.BlockSpec(memory_space=pl.ANY)
    dma = pltpu.SemaphoreType.DMA
    V = pltpu.VMEM
    return tuple(
        pl.pallas_call(
            functools.partial(kernel, groups, spans, frames_here),
            out_shape=(
                jax.ShapeDtypeStruct((rows, q_width), BF),
                jax.ShapeDtypeStruct((rows, c_width), BF),
            ),
            in_specs=[vmem] * 8 + [hbm] * 5,
            out_specs=(vmem, vmem),
            scratch_shapes=[
                V((width, width), BF),
                V((groups, width // groups, width), BF),
                V((width, model), BF),
                V(query_weight.shape, BF),
                V(cache_weight.shape, BF),
                V((4 * patches_here, width), BF),
                V((cells, width), BF),
                V((4 * patches_here, width), BF),
                V((max(4, frames_here) * patches_here, rows), F32),
                V((rows, width), F32),
                V((groups, piece, width), BF),
                V((groups, piece, width), BF),
                V((groups, piece, width), BF),
                V((groups, rows, model), BF),
                V((groups, 8, rows), F32),
                V((rows, q_width), F32),
                V((rows, c_width), F32),
                V((q_heads, rows, HD), BF),
                V((spans, groups, rows, c_width), BF),
                V((q_heads, rows, HD), F32),
                V((q_heads, rows, HD), F32),
                V((q_heads, rows, HD), F32),
                dma((5,)),
                dma((2,)),
                dma((2,)),
                dma((groups,)),
                dma((groups,)),
                dma((groups,)),
                dma((groups,)),
                dma((spans,)),
                dma((spans,)),
                dma((3 + spans, 4, chips)),
            ],
            compiler_params=pltpu.CompilerParams(
                collective_id=0, has_side_effects=True, vmem_limit_bytes=60 * 1024 * 1024
            ),
        )(
            features.reshape(cells, width),
            queries,
            coords,
            cosine,
            sine,
            norm_gain[None],
            query_bias[None],
            cache_bias[None],
            value_weight,
            output_weight,
            project_weight,
            query_weight,
            cache_weight,
        )
    )


def solution(mesh):
    return jax.shard_map(
        local,
        mesh=mesh,
        in_specs=(
            P(("dp", "tm"), "mp", None),
            P(("dp", "tm"), None),
            P(("dp", "tm")),
            P(("dp", "tm")),
            P(("dp", "tm"), None, None),
            P(None, ("dp", "tm"), None, None),
            P(),
            P(),
            P(),
            P("mp", None),
            P(None, "mp"),
            P("mp"),
            P(None, "mp"),
            P("mp"),
            P(None, "mp"),
            P("mp"),
        ),
        out_specs=(P(("dp", "tm"), "mp"), P(("dp", "tm"), "mp")),
        check_vma=False,
    )
```

time: 502 us -> 101 us (0.20); the launches traced: 494 us -> 101 us
  local copies, waits for them, and re-layouts: 293 us -> 6.64 us
  Pallas kernels: 0 us -> 87.6 us
  waiting for transfers between devices: 81.7 us -> 0 us
  blocking collectives: 40.3 us -> 0 us
  matrix products: 27.4 us -> 1.31 us
  other arithmetic: 24.5 us -> 4.42 us
  between operations: 14.7 us -> 0.72 us
  starting transfers between devices: 11.6 us -> 0 us
    gather x10 -> x0, local copies, waits for them, and re-layouts: 245 us -> none  [the longest x8 241 us: local(): picked = lookup[local_frame * patch_total + patch_id, head_lane]]
    pallas_call x0 -> x1, Pallas kernels: none -> 87.6 us  [local(): pl.pallas_call(functools.partial(kernel, groups, spans, frames_here), out...]
    psum x1 -> x0, waiting for transfers between devices: 37.8 us -> none  [local(): head_mix = lax.psum(head_terms, 'mp')]
    all_gather x3 -> x0, blocking collectives: 34.1 us -> none  [the longest x1 13.7 us: local(): lax.all_gather(key_rows, 'tm', axis=0, tiled=True)]
    dot_general x10 -> x1, matrix products: 27.4 us -> 1.31 us  [local(): jnp.dot(queries, point_weight, preferred_element_type=F32) + point_bias]
    all_to_all x1 -> x0, waiting for transfers between devices: 23.4 us -> none  [local(): lax.all_to_all(projected, 'mp', split_axis=2, concat_axis=1, tiled=True)]
    all_gather x1 -> x0, waiting for transfers between devices: 20.4 us -> none  [local(): shard_piece = lax.all_gather(normed, 'mp', axis=1, tiled=True)]
    reduce_sum x7 -> x1, other arithmetic: 16.5 us -> 0.03 us  [local(): share = jax.nn.softmax(logits.reshape(rows, AH, POINTS), axis=-1)]
  transfers between devices with their start and end apart: 5 -> 0, of which waited for: 3 -> 0; matrix products, arithmetic and copies ran while one was open for 4% -> 0% of each run, Pallas kernels for 0% -> 0%
where the time goes in v1:
time: 101 us
  Pallas kernels  87.6 us (87%)
  local copies, waits for them, and re-layouts  6.64 us (7%)
  other arithmetic  4.42 us (4%)
  matrix products  1.31 us (1%)
    pallas_call x1, Pallas kernels, local(): pl.pallas_call(functools.partial(kernel, groups, spans, frames_here), out...  87.6 us
    unnamed x4, local copies, waits for them, and re-layouts  3.34 us

profile of v1, /device:TPU:27, one launch (start us, length us, event | category | flops | bytes accessed | tf_op | source)
XLA Modules:
  0.0 100.7 jit_solution(16767075607597906509)
XLA Ops:
  0.6 0.0 copy-start
  0.7 0.7 convert_element_type.16
  1.4 0.7 fusion.2
  2.1 1.3 %broadcast_in_dim.7.query_bias = f32[1,768]{1,0:T(1,128)} reshape(f32[768]{0:T(1024)} %param.29) | data formatting | bytes 6144 | tf_op jit(solution)/shard_map/broadcast_in_dim | solution.py:528
  3.3 1.3 %broadcast_in_dim.6.gain = f32[1,896]{1,0:T(1,128)} reshape(f32[896]{0:T(1024)} %param.27) | data formatting | bytes 7168 | tf_op jit(solution)/shard_map/broadcast_in_dim | solution.py:527
  4.6 0.8 add_bitcast_fusion
  5.4 0.0 copy-done
  5.4 1.3 %convolution_add_fusion = f32[256,32]{0,1:T(8,128)S(1)} fusion(bf16[256,1024]{1,0:T(8,128)(2,1)} %queries.1, bf16[1024,32]{0,1:T(8,128)(2,1)S(1)} %copy-done, f32[32]{0:T(128)} %param.24), kind=kOutput, calls=%fused_computation | convolution fusion | flops 16785408 | bytes 622720 | tf_op jit(solution)/shard_map/dot_general | solution.py:451
  6.8 0.8 slice_add_fusion.1
  7.7 0.7 reshape.50.coords
  8.4 0.5 fusion
  8.9 0.8 pad_maximum_fusion
  9.7 87.6 %shard_map.167 = (bf16[256,768]{1,0:T(8,128)(2,1)}, bf16[256,256]{1,0:T(8,128)(2,1)}) custom-call(bf16[576,1024]{1,0:T(8,128)(2,1)} %bitcast.12, bf16[256,1024]{1,0:T(8,128)(2,1)} %queries.1, f32[8,16,256]{2,1,0:T(8,128)} %reshape.50.coords, f32[256,128]{1,0:T(8,128)} %get-tuple-element.10.cosine, f32[256,128]{1,0:T(8,128)} %get-tuple-element.11.sine, ...), custom_call_target="tpu_custom_call" | custom-call | tf_op jit(solution)/shard_map/pallas_call | solution.py:476
  97.3 1.8 %copy.21 = bf16[256,768]{1,0:T(8,128)(2,1)} copy(bf16[256,768]{1,0:T(8,128)(2,1)} %get-tuple-element.14) | data formatting | bytes 786432
  99.1 1.6 %copy.22 = bf16[256,256]{1,0:T(8,128)(2,1)} copy(bf16[256,256]{1,0:T(8,128)(2,1)} %get-tuple-element.15) | data formatting | bytes 262144
  (8 shorter events, 0.1 us)
Async XLA Ops:
  0.6 4.7 %copy-start = (bf16[1024,32]{0,1:T(8,128)(2,1)S(1)}, bf16[1024,32]{0,1:T(8,128)(2,1)}, u32[]{:S(2)}) copy-start(bf16[1024,32]{0,1:T(8,128)(2,1)} %param.23) | copy-start | bytes 196612
